TPU v7x, 32 devices: a whole 2x2x4 slice. The times are simulated.
32 devices in a mesh: expert: 4 (over z), vocab: 2 (over x), batch: 4 (over y, core).
Axes of the slice: x: 2, y: 2, z: 4, core: 2. Of those that a mesh axis runs over, the one named last changes fastest.
Arguments:
- resid: bfloat16 [4, 64, 6144], P('batch', ('expert', 'vocab')), may hold values from -6 to 6
- moe_gain: float32 [6144], replicated, may hold values from 0.25 to 2.5
- final_gain: float32 [6144], replicated, may hold values from 0.5 to 1.5
- router: bfloat16 [6144, 4], replicated, may hold values from -0.078125 to 0.078125
- w_gate: bfloat16 [4, 6144, 8192], P('expert', None, ('vocab', 'batch')), may hold values from -0.078125 to 0.078125
- w_up: bfloat16 [4, 6144, 8192], P('expert', None, ('vocab', 'batch')), may hold values from -0.078125 to 0.078125
- w_down: bfloat16 [4, 8192, 6144], P('expert', ('vocab', 'batch')), may hold values from -0.0625 to 0.0625
- lm_head: bfloat16 [16384, 6144], P(('expert', 'vocab')), may hold values from -6 to 6
- expert_ids: int32 [4, 64, 2], P('batch', ('expert', 'vocab')), may hold values from 0 to 3, all different within a row; in each aligned block of 8 rows (0 to 7, 8 to 15, ..., all dimensions but the last counted through in order) at most 5 rows name the same one
- target_ids: int32 [4, 64], P('batch'), may hold values from 0 to 16383
- choice_len: int32 [4, 8], P('batch'), may hold values from 1 to 32, 64 in all within a row
- choice_question: int32 [4, 8], P('batch'), may hold values from 0 to 1, as said below
Outputs:
- token_logprob: float32 [4, 64], P('batch', ('expert', 'vocab'))
- choice_prob: float32 [4, 8], P('batch')
Inputs may be any that keep to these rules, and one draw needn't show every extreme that they name: `expert_ids`: A token's 2 experts differ; the rows of one device name each expert at most 5 times. `choice_len`: each group's lengths sum to 64. `choice_question`: in each group every question number appears exactly four times.
All inputs are finite; a program needn't handle non-finite values.
Results may differ from a plain program's by a relative error of at most 0.019.
Values may be sent and summed in bfloat16 or wider, within the bound.
A program may use at most 128 MiB of HBM per device.

v0:
```python
import jax
import jax.numpy as jnp
from jax import lax
from jax.sharding import PartitionSpec as P

epsilon = 1e-05


def joined(array, axis, combine):
    everything = jax.tree.map(lambda part: lax.all_gather(part, axis), array)
    leading = jax.tree.map(lambda part: part[0], everything)

    def lap(k, so_far):
        return combine(so_far, jax.tree.map(lambda part: part[k], everything))

    return lax.fori_loop(1, lax.axis_size(axis), lap, leading)


def rms_scale(values, gain):
    mean_square = jnp.mean(values * values, axis=-1, keepdims=True)
    return values * lax.rsqrt(mean_square + epsilon) * gain


def route_gates(router_logit, route_ids):
    expert_count = router_logit.shape[1]
    matches = route_ids[:, :, None] == jnp.arange(expert_count, dtype=jnp.int32)[None, None, :]
    picked = jnp.sum(jnp.where(matches, router_logit[:, None, :], 0.0), axis=2)
    return 1.0 / jnp.sum(jnp.exp(picked[:, None, :] - picked[:, :, None]), axis=2)


def expand_rows(block_rows, gate_cols, up_cols):
    gate_part = jnp.dot(block_rows, gate_cols, preferred_element_type=jnp.float32)
    up_part = jnp.dot(block_rows, up_cols, preferred_element_type=jnp.float32)
    return (jax.nn.silu(gate_part) * up_part).astype(jnp.bfloat16)


def choice_member(lengths, positions):
    ends = jnp.cumsum(lengths, dtype=jnp.int32)
    starts = ends - lengths
    return (positions[None, :] >= starts[:, None]) & (positions[None, :] < ends[:, None])


def choice_softmax(choice_total, lengths, questions):
    average = choice_total / lengths.astype(jnp.float32)
    same_question = questions[:, None] == questions[None, :]
    question_top = jnp.max(jnp.where(same_question, average[None, :], -jnp.inf), axis=1)
    raised = jnp.exp(average - question_top)
    denominator = jnp.sum(jnp.where(same_question, raised[None, :], 0.0), axis=1)
    return raised / denominator


def merge_stats(first, second):
    top_value = jnp.maximum(first[0], second[0])
    summed = first[1] * jnp.exp(first[0] - top_value) + second[1] * jnp.exp(second[0] - top_value)
    return (top_value, summed, first[2] + second[2])


def on_device(
    resid,
    moe_gain,
    final_gain,
    router,
    w_gate,
    w_up,
    w_down,
    lm_head,
    expert_ids,
    target_ids,
    choice_len,
    choice_question,
):
    stream = resid[0].astype(jnp.float32)
    token_count, model_width = stream.shape
    normed_in = rms_scale(stream, moe_gain).astype(jnp.bfloat16)
    router_logit = jnp.dot(normed_in, router, preferred_element_type=jnp.float32)
    route_ids = expert_ids[0]
    route_count = route_ids.shape[1]
    gate_weights = route_gates(router_logit, route_ids)
    expert_count = lax.axis_size("expert")
    bucket_size = max(2, (token_count * route_count + expert_count - 1) // expert_count + 1)
    flat_ids = route_ids.reshape(-1)
    expert_match = (flat_ids[:, None] == jnp.arange(expert_count, dtype=jnp.int32)[None, :]).astype(
        jnp.int32
    )
    earlier = jnp.cumsum(expert_match, axis=0, dtype=jnp.int32) - expert_match
    slot_index = flat_ids * bucket_size + jnp.sum(earlier * expert_match, axis=1)
    slot_match = (
        slot_index[:, None] == jnp.arange(expert_count * bucket_size, dtype=jnp.int32)[None, :]
    ).astype(jnp.float32)
    slot_match = slot_match.reshape(token_count, route_count, -1)
    dispatch = jnp.sum(slot_match, axis=1).astype(jnp.bfloat16)
    combine_weights = jnp.sum(slot_match * gate_weights[:, :, None], axis=1)
    buckets = lax.dot_general(
        dispatch, normed_in, (((0,), (0,)), ((), ())), preferred_element_type=jnp.float32
    )
    buckets = buckets.astype(jnp.bfloat16).reshape(expert_count, bucket_size, model_width)
    gate_cols = w_gate[0]
    up_cols = w_up[0]
    down_rows = w_down[0]
    arrived = lax.all_to_all(buckets, "expert", split_axis=0, concat_axis=0, tiled=True).reshape(
        -1, model_width
    )
    hidden = expand_rows(
        lax.all_gather(arrived, ("vocab", "batch"), axis=0, tiled=True), gate_cols, up_cols
    )
    expert_sum = lax.psum_scatter(
        jnp.dot(hidden, down_rows, preferred_element_type=jnp.float32).astype(jnp.bfloat16),
        ("vocab", "batch"),
        scatter_dimension=0,
        tiled=True,
    )
    outgoing = expert_sum.reshape(expert_count, bucket_size, model_width)
    returned = lax.all_to_all(outgoing, "expert", split_axis=0, concat_axis=0, tiled=True)
    returned_rows = returned.reshape(-1, model_width).astype(jnp.float32)
    mixed_rows = stream + jnp.dot(combine_weights, returned_rows, precision=lax.Precision.HIGHEST)
    normed_out = rms_scale(mixed_rows, final_gain).astype(jnp.bfloat16)
    head_index = lax.axis_index(("expert", "vocab"))
    vocab_share = lm_head.shape[0]
    vocab_ids = jnp.arange(vocab_share, dtype=jnp.int32) + head_index * vocab_share
    targets = target_ids[0]
    group_tokens = targets.shape[0]
    logits = lax.dot_general(
        lax.all_gather(normed_out, ("expert", "vocab"), axis=0, tiled=True),
        lm_head,
        (((1,), (1,)), ((), ())),
        preferred_element_type=jnp.float32,
    )
    block_top = jnp.max(logits, axis=1)
    block_sum = jnp.sum(jnp.exp(logits - block_top[:, None]), axis=1)
    block_hit = jnp.sum(jnp.where(targets[:, None] == vocab_ids[None, :], logits, 0.0), axis=1)
    fresh = (block_top, block_sum, block_hit)
    largest, spread_sum, chosen = tuple((fresh[slot] for slot in range(3)))
    lengths = choice_len[0]
    questions = choice_question[0]
    own_first = head_index * token_count
    group_positions = jnp.arange(group_tokens, dtype=jnp.int32)
    best, summed, target_sum = joined(
        (largest, spread_sum, chosen), ("expert", "vocab"), merge_stats
    )
    group_logprob = target_sum - (best + jnp.log(summed))
    choice_total = jnp.sum(
        jnp.where(choice_member(lengths, group_positions), group_logprob[None, :], 0.0), axis=1
    )
    own_logprob = lax.dynamic_slice_in_dim(group_logprob, own_first, token_count, 0)
    choice_prob = choice_softmax(choice_total, lengths, questions)
    return (own_logprob.reshape(1, -1), choice_prob.reshape(1, -1))


def solution(mesh):
    return jax.shard_map(
        on_device,
        mesh=mesh,
        in_specs=(
            P("batch", ("expert", "vocab"), None),
            P(),
            P(),
            P(),
            P("expert", None, ("vocab", "batch")),
            P("expert", None, ("vocab", "batch")),
            P("expert", ("vocab", "batch"), None),
            P(("expert", "vocab"), None),
            P("batch", ("expert", "vocab"), None),
            P("batch", None),
            P("batch", None),
            P("batch", None),
        ),
        out_specs=(P("batch", ("expert", "vocab")), P("batch", None)),
        check_vma=False,
    )
```

profile of v0, /device:TPU:0, one launch (start us, length us, event | category | flops | bytes accessed | tf_op | source)
XLA Modules:
  0.0 217.9 jit_solution(4408126058935041288)
XLA Ops:
  7.2 0.0 copy-start
  7.2 0.0 all-gather.6.cloned.1.call-start
  7.2 0.8 copy.29
  8.0 0.1 eq.72
  8.1 0.1 fusion.32
  8.2 0.2 select_reduce_fusion.2
  8.4 0.1 reduce_sum.106
  8.4 0.1 copy.30
  8.5 0.7 multiply_add_fusion
  9.2 1.1 fusion.26
  10.3 0.0 copy-done
  10.3 1.1 fusion.30
  11.4 0.7 select_reduce_fusion.4
  12.2 0.1 convert_reduce_fusion
  12.2 1.2 convolution_convert_fusion
  13.4 0.1 reshape.107
  13.6 17.8 %all_to_all.10 = bf16[4,5,6144]{2,1,0:T(8,128)(2,1)S(1)} all-to-all(bf16[4,5,6144]{2,1,0:T(8,128)(2,1)S(1)} %reshape.107), channel_id=1, replica_groups=mesh['expert'=4,'vocab'=2,'batch'=4] {'expert'}, dimensions={0} | all-to-all | bytes 491520 | tf_op jit(solution)/shard_map/all_to_all | solution.py:100
  31.4 0.8 reshape.134
  32.2 0.0 all-gather.6.cloned.1.call-update
  32.2 28.1 %all-gather.6.cloned.1.call-done = bf16[8,20,6144]{2,1,0:T(8,128)(2,1)} async-done(((bf16[1,20,6144]{2,1,0:T(8,128)(2,1)}), bf16[8,20,6144]{2,1,0:T(8,128)(2,1)}) %all-gather.6.cloned.1.call-update) | async-done | bytes 1966096 | tf_op jit(solution)/shard_map/all_gather | solution.py:104
  60.4 2.6 %reshape.135 = bf16[160,6144]{1,0:T(8,128)(2,1)S(1)} reshape(bf16[8,20,6144]{2,1,0:T(8,128)(2,1)} %all-gather.6.cloned.1.call-done) | data formatting | bytes 3932160
  63.0 6.8 %fusion.12 = f32[160,1024]{1,0:T(8,128)S(1)} fusion(bf16[160,6144]{1,0:T(8,128)(2,1)S(1)} %reshape.135, bf16[1,6144,1024]{2,1,0:T(8,128)(2,1)} %param.18), kind=kOutput, calls=%fused_computation.14 | convolution fusion | flops 2013265920 | bytes 15204352 | tf_op jit(solution)/shard_map/dot_general | solution.py:32
  69.8 0.0 copy-start.5
  69.8 0.0 copy-start.7
  69.8 0.0 copy-start.8
  69.8 0.0 copy-start.2
  69.8 0.0 copy-start.3
  69.8 13.8 %fusion.14 = bf16[160,6144]{1,0:T(8,128)(2,1)} fusion(bf16[1,1024,6144]{2,1,0:T(8,128)(2,1)} %param.20, bf16[160,6144]{1,0:T(8,128)(2,1)S(1)} %reshape.135, bf16[1,6144,1024]{2,1,0:T(8,128)(2,1)} %param.19, f32[160,1024]{1,0:T(8,128)S(1)} %fusion.12), kind=kOutput, calls=%fused_computation.16 | convolution fusion | flops 4028497920 | bytes 29753344 | tf_op jit(solution)/shard_map/dot_general | solution.py:107
  83.6 27.0 %fusion = bf16[24,6144]{1,0:T(8,128)(2,1)S(1)} fusion(bf16[160,6144]{1,0:T(8,128)(2,1)} %fusion.14), kind=kCustom, calls=%all-reduce-scatter | all-reduce-scatter fusion | flops 1179649 | bytes 2261504
  110.7 5.9 %collective-permute-start = (bf16[24,6144]{1,0:T(8,128)(2,1)S(1)}, bf16[24,6144]{1,0:T(8,128)(2,1)S(1)}, u32[]{:S(2)}, u32[]{:S(2)}) collective-permute-start(bf16[24,6144]{1,0:T(8,128)(2,1)S(1)} %fusion), channel_id=1, source_target_pairs={{0,1},{1,2},{2,3},{3,4},{4,5},{5,6},{6,7},{8,9},{9,10},{10,11},{11... | collective-permute-start | bytes 884744
  116.6 4.2 %collective-permute-start.1 = (bf16[4,6144]{1,0:T(4,128)(2,1)S(1)}, bf16[4,6144]{1,0:T(4,128)(2,1)S(1)}, u32[]{:S(2)}, u32[]{:S(2)}) collective-permute-start(bf16[4,6144]{1,0:T(4,128)(2,1)S(1)} %slice.15), channel_id=1, source_target_pairs={{0,2},{1,3},{2,4},{3,5},{4,6},{5,7},{8,10},{9,11},{10,12},{11,13},... | collective-permute-start | bytes 147464
  120.9 0.0 copy-done.5
  120.9 0.6 dynamic-slice.7
  122.1 0.9 collective-permute-done.1
  123.0 0.0 collective-permute-done
  123.0 1.1 concatenate
  124.1 0.1 constant_dynamic-slice_fusion.3
  124.2 0.8 reshape.109
  125.0 4.6 %all-to-all-start.1 = ((bf16[4,5,6144]{2,1,0:T(8,128)(2,1)}), bf16[4,5,6144]{2,1,0:T(8,128)(2,1)S(1)}, u32[]{:S(2)}, u32[]{:S(2)}) async-start(bf16[4,5,6144]{2,1,0:T(8,128)(2,1)} %reshape.109), calls=%async_computation.1 | async-start | bytes 786432 | tf_op jit(solution)/shard_map/all_to_all | solution.py:113
  129.6 0.2 reduce-window.7
  129.8 0.0 copy-done.8
  129.8 0.6 dynamic-slice
  131.1 11.2 %all-to-all-done.1 = bf16[4,5,6144]{2,1,0:T(8,128)(2,1)S(1)} async-done(((bf16[4,5,6144]{2,1,0:T(8,128)(2,1)}), bf16[4,5,6144]{2,1,0:T(8,128)(2,1)S(1)}, u32[]{:S(2)}, u32[]{:S(2)}) %all-to-all-start.1) | async-done | bytes 245792 | tf_op jit(solution)/shard_map/all_to_all | solution.py:113
  142.2 0.1 reshape.110
  142.3 0.4 multiply_reduce_fusion
  142.8 0.1 multiply_convert_fusion
  142.9 0.0 copy-start.1
  142.9 32.4 %all_gather.25 = bf16[64,6144]{1,0:T(8,128)(2,1)S(1)} all-gather(bf16[8,6144]{1,0:T(8,128)(2,1)S(1)} %multiply_convert_fusion), channel_id=1, replica_groups=mesh['expert'=4,'vocab'=2,'batch'=4] {'expert','vocab'}, dimensions={0}, use_global_device_ids=true | all-gather | bytes 884736 | tf_op jit(solution)/shard_map/all_gather | solution.py:123
  175.3 12.6 %fusion.41 = (f32[64]{0:T(128)S(1)}, f32[64,2048]{1,0:T(8,128)S(1)}) fusion(bf16[64,6144]{1,0:T(8,128)(2,1)S(1)} %all_gather.25, bf16[2048,6144]{1,0:T(8,128)(2,1)} %param.21), kind=kOutput, calls=%fused_computation.65 | convolution fusion | flops 1610743808 | bytes 26476800 | tf_op jit(solution)/shard_map/dot_general | solution.py:122
  187.9 0.2 dynamic-update-slice
  188.1 0.3 select_reduce_fusion
  188.4 0.2 dynamic-update-slice.2
  188.6 0.2 dynamic-update-slice.1
  188.9 20.0 %all-reduce.5 = (f32[512]{0:T(512)S(1)}, f32[512]{0:T(512)S(1)}, f32[512]{0:T(512)S(1)}) all-reduce(f32[512]{0:T(512)S(1)} %dynamic-update-slice, f32[512]{0:T(512)S(1)} %dynamic-update-slice.1, f32[512]{0:T(512)S(1)} %dynamic-update-slice.2), channel_id=2, replica_groups=mesh['expert'=4,'vocab'=2,'batch'=4] {'expert','vocab'}, use_global_device_ids=true, to_apply=%add | all-reduce | flops 1536 | bytes 12288
  208.8 0.1 reshape.116
  208.9 0.1 reshape.117
  209.0 0.1 reshape.118
  209.0 0.3 while.19
  209.4 0.2 select_reduce_fusion.3
  209.5 0.0 copy-done.4
  209.6 0.2 fusion.33
  209.7 0.2 fusion.34
  209.9 0.5 bitcast_divide_fusion
  210.5 0.6 dynamic-slice_bitcast_fusion
  (31 shorter events, 0.4 us)
Async XLA Ops:
  7.2 3.1 %copy-start = (bf16[6144,4]{0,1:T(4,128)(2,1)S(1)}, bf16[6144,4]{0,1:T(4,128)(2,1)}, u32[]{:S(2)}) copy-start(bf16[6144,4]{0,1:T(4,128)(2,1)} %param.17) | copy-start | bytes 147460
  7.2 53.2 %all-gather.6.cloned.1.call-start = ((), (), s32[]{:S(2)}) async-start(), calls=%async_computation.2 | async-start | bytes 2654208 | tf_op jit(solution)/shard_map/all_gather | solution.py:104
  69.8 51.1 %copy-start.5 = (u32[32]{0:T(128)S(1)}, u32[32]{0:T(128)}, u32[]{:S(2)}) copy-start(u32[32]{0:T(128)} %constant.108) | copy-start | bytes 388
  69.8 59.9 %copy-start.7 = (s32[1,8]{1,0:T(1,128)S(1)}, s32[1,8]{1,0:T(1,128)}, u32[]{:S(2)}) copy-start(s32[1,8]{1,0:T(1,128)} %param.24) | copy-start | bytes 100
  69.8 60.0 %copy-start.8 = (u32[32]{0:T(128)S(1)}, u32[32]{0:T(128)}, u32[]{:S(2)}) copy-start(u32[32]{0:T(128)} %constant.90) | copy-start | bytes 388
  69.8 72.5 %copy-start.2 = (bf16[1,8,6144]{2,1,0:T(8,128)(2,1)S(1)}, bf16[1,8,6144]{2,1,0:T(8,128)(2,1)}, u32[]{:S(2)}) copy-start(bf16[1,8,6144]{2,1,0:T(8,128)(2,1)} %param.14) | copy-start | bytes 294916
  69.8 72.9 %copy-start.3 = (f32[6144]{0:T(1024)S(1)}, f32[6144]{0:T(1024)}, u32[]{:S(2)}) copy-start(f32[6144]{0:T(1024)} %param.16) | copy-start | bytes 73732
  110.7 12.3 %collective-permute-start = (bf16[24,6144]{1,0:T(8,128)(2,1)S(1)}, bf16[24,6144]{1,0:T(8,128)(2,1)S(1)}, u32[]{:S(2)}, u32[]{:S(2)}) collective-permute-start(bf16[24,6144]{1,0:T(8,128)(2,1)S(1)} %fusion), channel_id=1, source_target_pairs={{0,1},{1,2},{2,3},{3,4},{4,5},{5,6},{6,7},{8,9},{9,10},{10,11},{11... | collective-permute-start | bytes 884744
  116.6 6.4 %collective-permute-start.1 = (bf16[4,6144]{1,0:T(4,128)(2,1)S(1)}, bf16[4,6144]{1,0:T(4,128)(2,1)S(1)}, u32[]{:S(2)}, u32[]{:S(2)}) collective-permute-start(bf16[4,6144]{1,0:T(4,128)(2,1)S(1)} %slice.15), channel_id=1, source_target_pairs={{0,2},{1,3},{2,4},{3,5},{4,6},{5,7},{8,10},{9,11},{10,12},{11,13},... | collective-permute-start | bytes 147464
  125.0 17.2 %all-to-all-start.1 = ((bf16[4,5,6144]{2,1,0:T(8,128)(2,1)}), bf16[4,5,6144]{2,1,0:T(8,128)(2,1)S(1)}, u32[]{:S(2)}, u32[]{:S(2)}) async-start(bf16[4,5,6144]{2,1,0:T(8,128)(2,1)} %reshape.109), calls=%async_computation.1 | async-start | bytes 786432 | tf_op jit(solution)/shard_map/all_to_all | solution.py:113
  142.9 68.2 %copy-start.1 = (bf16[6144,4]{0,1:T(4,128)(2,1)S(1)}, bf16[6144,4]{0,1:T(4,128)(2,1)}, u32[]{:S(2)}) copy-start(bf16[6144,4]{0,1:T(4,128)(2,1)} %param.17) | copy-start | bytes 147460
  175.3 12.8 %copy-start.6 = (s32[1,64]{1,0:T(1,128)S(1)}, s32[1,64]{1,0:T(1,128)}, u32[]{:S(2)}) copy-start(s32[1,64]{1,0:T(1,128)} %param.23) | copy-start | bytes 772
  175.3 34.3 %copy-start.4 = (s32[1,8]{1,0:T(1,128)S(1)}, s32[1,8]{1,0:T(1,128)}, u32[]{:S(2)}) copy-start(s32[1,8]{1,0:T(1,128)} %param.25) | copy-start | bytes 100
Sparse Core Ops, SparseCore 0:
  32.4 27.9 all-gather.5
where the time goes:
time: 219 us; the launch traced here: 218 us
  blocking collectives  97.2 us (44%)
  waiting for transfers between devices  40.2 us (18%)
  matrix products  35.9 us (16%)
  between operations  15.6 us (7%)
  starting transfers between devices  14.8 us (7%)
  local copies, waits for them, and re-layouts  9.43 us (4%)
  other arithmetic  4.75 us (2%)
    unnamed x2, blocking collectives  47 us
    all_gather x1, blocking collectives, on_device(): lax.all_gather(normed_out, ('expert', 'vocab'), axis=0, tiled=True)  32.4 us
    all_gather x1, waiting for transfers between devices, on_device(): lax.all_gather(arrived, ('vocab', 'batch'), axis=0, tiled=True)  28.1 us
    all_to_all x1, blocking collectives, on_device(): lax.all_to_all(buckets, 'expert', split_axis=0, concat_axis=0, tiled=True)  17.8 us
    dot_general x1, matrix products, on_device(): jnp.dot(hidden, down_rows, preferred_element_type=jnp.float32)  13.8 us
    dot_general x1, matrix products, on_device(): lax.dot_general(lax.all_gather(normed_out, ('expert', 'vocab'), axis=0, t...  12.6 us
    all_to_all x1, waiting for transfers between devices, on_device(): lax.all_to_all(outgoing, 'expert', split_axis=0, concat_axis=0, tiled=True)  11.2 us
    unnamed x2, starting transfers between devices  10.2 us
  transfers between devices with their start and end apart: 4, of which 3 were waited for; matrix products, arithmetic and copies ran while one was open for 1% of the time, Pallas kernels for 0%

commit v1 on v0

--- a/solution.py
+++ b/solution.py
@@ -1,6 +1,10 @@
+import functools
+
 import jax
 import jax.numpy as jnp
 from jax import lax
+from jax.experimental import pallas as pl
+from jax.experimental.pallas import tpu as pltpu
 from jax.sharding import PartitionSpec as P
 
 epsilon = 1e-05
@@ -146,9 +150,465 @@
     return (own_logprob.reshape(1, -1), choice_prob.reshape(1, -1))
 
 
+MESH = pl.DeviceIdType.MESH
+VMEM_BYTES = 67043328
+COLUMN_CHUNKS = 4
+
+
+def greet(partners):
+    barrier = pltpu.get_barrier_semaphore()
+    for partner in partners:
+        pl.semaphore_signal(barrier, inc=1, device_id=partner, device_id_type=MESH)
+    pl.semaphore_wait(barrier, len(partners))
+
+
+def push(src, dst, send_sem, recv_sem, partner):
+    return pltpu.make_async_remote_copy(
+        src_ref=src,
+        dst_ref=dst,
+        send_sem=send_sem,
+        recv_sem=recv_sem,
+        device_id=partner,
+        device_id_type=MESH,
+    )
+
+
+def experts_kernel(
+    ne,
+    nv,
+    nb,
+    own_ref,
+    resid_ref,
+    gates_ref,
+    gain_ref,
+    wg_hbm,
+    wu_hbm,
+    wd_hbm,
+    out_ref,
+    wg,
+    wu,
+    wd,
+    zin,
+    xs,
+    hid,
+    part,
+    rpair,
+    rchip,
+    zs,
+    zo,
+    w_sem,
+    z_send,
+    z_recv,
+    c_send,
+    c_recv,
+    p_send,
+    p_recv,
+    rp_send,
+    rp_recv,
+    rc_send,
+    rc_recv,
+    rz_send,
+    rz_recv,
+):
+    e, v, b = lax.axis_index("expert"), lax.axis_index("vocab"), lax.axis_index("batch")
+    half = nb // 2
+    chips = nv * half
+    core = lax.rem(b, 2)
+    other = 1 - core
+    chip = v * half + b // 2
+    tokens, width = own_ref.shape
+    block = ne * tokens
+
+    def at_expert(k):
+        return (lax.rem(e + k, ne), v, b)
+
+    def at_chip(k):
+        c = lax.rem(chip + k, chips)
+        return (e, c // half, lax.rem(c, half) * 2 + core)
+
+    mate = (e, v, b + 1 - 2 * core)
+
+    loads = [
+        pltpu.make_async_copy(src, dst, w_sem.at[i])
+        for i, (src, dst) in enumerate(((wg_hbm.at[0], wg), (wu_hbm.at[0], wu), (wd_hbm.at[0], wd)))
+    ]
+    for load in loads:
+        load.start()
+    greet(
+        [at_expert(k) for k in range(1, ne)] + [at_chip(k) for k in range(1, chips)] + [mate]
+    )
+
+    z_copies = [
+        push(own_ref, zin.at[e], z_send.at[k], z_recv.at[k], at_expert(k)) for k in range(1, ne)
+    ]
+    for copy in z_copies:
+        copy.start()
+    zin[e] = own_ref[...]
+    for copy in z_copies:
+        copy.wait_recv()
+    xs[core, chip] = (
+        zin[...].astype(jnp.float32).reshape(block, width).astype(jnp.bfloat16)
+    )
+
+    c_copies = [
+        push(
+            xs.at[core, chip], xs.at[core, chip], c_send.at[k], c_recv.at[k], at_chip(k)
+        )
+        for k in range(1, chips)
+    ]
+    p_copies = []
+    for k in range(chips):
+        c = lax.rem(chip + chips - k, chips)
+        p_copies.append(push(xs.at[core, c], xs.at[core, c], p_send.at[k], p_recv.at[k], mate))
+    for copy in c_copies:
+        copy.start()
+    p_copies[0].start()
+    for k in range(1, chips):
+        c_copies[k - 1].wait_recv()
+        p_copies[k].start()
+    for copy in p_copies:
+        copy.wait_recv()
+
+    rows = 2 * chips * block
+    loads[0].wait()
+    loads[1].wait()
+    hidden_width = wg.shape[1]
+    tile = min(256, hidden_width)
+
+    @pl.loop(0, hidden_width // tile)
+    def _(i):
+        cols = pl.ds(pl.multiple_of(i * tile, tile), tile)
+        x = xs[...].reshape(rows, width)
+        g = jnp.dot(x, wg[:, cols], preferred_element_type=jnp.float32)
+        u = jnp.dot(x, wu[:, cols], preferred_element_type=jnp.float32)
+        hid[:, cols] = (g / (1.0 + jnp.exp(-g)) * u).astype(jnp.bfloat16)
+
+    loads[2].wait()
+    chunk = width // COLUMN_CHUNKS
+    down_tile = 512 if chunk % 512 == 0 else 128
+    rp, rc, rz = [], [], []
+
+    def columns(j):
+        return pl.ds(j * chunk, chunk)
+
+    def down(j):
+        @pl.loop(0, chunk // down_tile)
+        def _(i):
+            cols = pl.ds(pl.multiple_of(j * chunk + i * down_tile, down_tile), down_tile)
+            y = jnp.dot(hid[...], wd[:, cols], preferred_element_type=jnp.float32)
+            part[:, :, :, cols] = y.astype(jnp.bfloat16).reshape(2, chips, block, down_tile)
+
+        copy = push(
+            part.at[other, :, :, columns(j)],
+            rpair.at[:, :, columns(j)],
+            rp_send.at[j],
+            rp_recv.at[j],
+            mate,
+        )
+        copy.start()
+        rp.append(copy)
+
+    def pair_sum(j):
+        rp[j].wait_recv()
+        total = part[core, :, :, columns(j)].astype(jnp.float32) + rpair[
+            :, :, columns(j)
+        ].astype(jnp.float32)
+        part[core, :, :, columns(j)] = total.astype(jnp.bfloat16)
+        for k in range(1, chips):
+            to = lax.rem(chip + k, chips)
+            copy = push(
+                part.at[core, to, :, columns(j)],
+                rchip.at[k - 1, :, columns(j)],
+                rc_send.at[j, k],
+                rc_recv.at[j, k],
+                at_chip(k),
+            )
+            copy.start()
+            rc.append(copy)
+
+    def plane_sum(j):
+        for k in range(1, chips):
+            rc[j * (chips - 1) + k - 1].wait_recv()
+        total = part[core, chip, :, columns(j)].astype(jnp.float32)
+        for k in range(1, chips):
+            total = total + rchip[k - 1, :, columns(j)].astype(jnp.float32)
+        zs[:, :, columns(j)] = total.reshape(ne, tokens, chunk).astype(jnp.bfloat16)
+        for k in range(1, ne):
+            to = lax.rem(e + k, ne)
+            copy = push(
+                zs.at[to, :, columns(j)],
+                zo.at[e, :, columns(j)],
+                rz_send.at[j, k],
+                rz_recv.at[j, k],
+                at_expert(k),
+            )
+            copy.start()
+            rz.append(copy)
+        zo[e, :, columns(j)] = zs[e, :, columns(j)]
+
+    for j in range(COLUMN_CHUNKS):
+        down(j)
+        if j >= 1:
+            pair_sum(j - 1)
+    pair_sum(COLUMN_CHUNKS - 1)
+    for j in range(COLUMN_CHUNKS):
+        plane_sum(j)
+    for copy in rz:
+        copy.wait_recv()
+    gates = gates_ref[...]
+    mixed = resid_ref[...].astype(jnp.float32)
+    for k in range(ne):
+        mixed = mixed + gates[:, k : k + 1] * zo[k].astype(jnp.float32)
+    scale = lax.rsqrt(jnp.mean(mixed * mixed, axis=-1, keepdims=True) + epsilon)
+    out_ref[...] = (mixed * scale * gain_ref[...]).astype(jnp.bfloat16)
+    for copy in z_copies + c_copies + p_copies + rp + rc + rz:
+        copy.wait_send()
+
+
+def experts_call(sizes, own, resid, gates, gain, w_gate, w_up, w_down):
+    ne, nv, nb = sizes
+    tokens, width = own.shape
+    hidden_width = w_gate.shape[2]
+    chips = nv * nb // 2
+    block = ne * tokens
+    bf16 = jnp.bfloat16
+    dma = pltpu.SemaphoreType.DMA
+    vm = pl.BlockSpec(memory_space=pltpu.VMEM)
+    anywhere = pl.BlockSpec(memory_space=pl.ANY)
+    n = COLUMN_CHUNKS
+    return pl.pallas_call(
+        functools.partial(experts_kernel, ne, nv, nb),
+        out_shape=jax.ShapeDtypeStruct((tokens, width), bf16),
+        in_specs=[vm, vm, vm, vm, anywhere, anywhere, anywhere],
+        out_specs=vm,
+        scratch_shapes=[
+            pltpu.VMEM((width, hidden_width), bf16),
+            pltpu.VMEM((width, hidden_width), bf16),
+            pltpu.VMEM((hidden_width, width), bf16),
+            pltpu.VMEM((ne, tokens, width), bf16),
+            pltpu.VMEM((2, chips, block, width), bf16),
+            pltpu.VMEM((2 * chips * block, hidden_width), bf16),
+            pltpu.VMEM((2, chips, block, width), bf16),
+            pltpu.VMEM((chips, block, width), bf16),
+            pltpu.VMEM((max(1, chips - 1), block, width), bf16),
+            pltpu.VMEM((ne, tokens, width), bf16),
+            pltpu.VMEM((ne, tokens, width), bf16),
+            dma((3,)),
+            dma((ne,)),
+            dma((ne,)),
+            dma((chips,)),
+            dma((chips,)),
+            dma((chips,)),
+            dma((chips,)),
+            dma((n,)),
+            dma((n,)),
+            dma((n, chips)),
+            dma((n, chips)),
+            dma((n, ne)),
+            dma((n, ne)),
+        ],
+        compiler_params=pltpu.CompilerParams(
+            collective_id=0, has_side_effects=True, vmem_limit_bytes=VMEM_BYTES - 2 * 1024 * 1024
+        ),
+        name="experts",
+    )(own, resid, gates, gain, w_gate, w_up, w_down)
+
+
+def head_kernel(
+    ne, nv, own_ref, target_ref, head_hbm, out_ref, head, ys, stats, h_sem, y_send, y_recv, s_send, s_recv
+):
+    e, v, b = lax.axis_index("expert"), lax.axis_index("vocab"), lax.axis_index("batch")
+    peers = ne * nv
+    me = e * nv + v
+    share, width = head.shape
+    tokens = own_ref.shape[0]
+    rows = peers * tokens
+    lanes = out_ref.shape[1]
+    tile = min(256, share)
+
+    def at(k):
+        p = lax.rem(me + k, peers)
+        return (p // nv, lax.rem(p, nv), b)
+
+    parts = h_sem.shape[0]
+    depth = share // parts
+    loads = [
+        pltpu.make_async_copy(
+            head_hbm.at[pl.ds(i * depth, depth)], head.at[pl.ds(i * depth, depth)], h_sem.at[i]
+        )
+        for i in range(parts)
+    ]
+    for load in loads:
+        load.start()
+    greet([at(k) for k in range(1, peers)])
+    copies = [
+        push(own_ref, ys.at[me], y_send.at[k], y_recv.at[k], at(k)) for k in range(1, peers)
+    ]
+    for copy in copies:
+        copy.start()
+    ys[me] = own_ref[...]
+    for copy in copies:
+        copy.wait_recv()
+    for load in loads:
+        load.wait()
+    y = ys[...].astype(jnp.float32).reshape(rows, width).astype(jnp.bfloat16)
+    targets = target_ref[...]
+
+    def lap(i, carry):
+        top, total, hit = carry
+        first = pl.multiple_of(i * tile, tile)
+        logits = lax.dot_general(
+            y,
+            head[pl.ds(first, tile), :],
+            (((1,), (1,)), ((), ())),
+            preferred_element_type=jnp.float32,
+        )
+        ids = lax.broadcasted_iota(jnp.int32, logits.shape, 1) + (me * share + first)
+        new_top = jnp.maximum(top, jnp.max(logits, axis=1, keepdims=True))
+        total = total * jnp.exp(top - new_top) + jnp.sum(
+            jnp.exp(logits - new_top), axis=1, keepdims=True
+        )
+        hit = hit + jnp.sum(jnp.where(ids == targets, logits, 0.0), axis=1, keepdims=True)
+        return new_top, total, hit
+
+    zero = jnp.zeros((rows, 1), jnp.float32)
+    top, total, hit = lax.fori_loop(
+        0, share // tile, lap, (jnp.full((rows, 1), -jnp.inf, jnp.float32), zero, zero)
+    )
+    eye = lax.broadcasted_iota(jnp.int32, (rows, lanes), 0) == lax.broadcasted_iota(
+        jnp.int32, (rows, lanes), 1
+    )
+
+    def laid(column):
+        return jnp.sum(jnp.where(eye, column, 0.0), axis=0, keepdims=True)
+
+    line = lax.broadcasted_iota(jnp.int32, (8, lanes), 0)
+    stats[me] = jnp.where(
+        line == 0, laid(top), jnp.where(line == 1, laid(total), jnp.where(line == 2, laid(hit), 0.0))
+    )
+    sends = [
+        push(stats.at[me], stats.at[me], s_send.at[k], s_recv.at[k], at(k)) for k in range(1, peers)
+    ]
+    for copy in sends:
+        copy.start()
+    for copy in sends:
+        copy.wait_recv()
+    every = stats[...]
+    best = jnp.max(every[:, 0:1, :], axis=0)
+    summed = jnp.sum(every[:, 1:2, :] * jnp.exp(every[:, 0:1, :] - best[None]), axis=0)
+    chosen = jnp.sum(every[:, 2:3, :], axis=0)
+    used = lax.broadcasted_iota(jnp.int32, (1, lanes), 1) < rows
+    logprob = chosen - (best + jnp.log(jnp.where(used, summed, 1.0)))
+    out_ref[...] = jnp.broadcast_to(logprob, out_ref.shape)
+    for copy in copies + sends:
+        copy.wait_send()
+
+
+def head_call(sizes, own, targets, lm_head):
+    ne, nv, nb = sizes
+    tokens, width = own.shape
+    peers = ne * nv
+    dma = pltpu.SemaphoreType.DMA
+    vm = pl.BlockSpec(memory_space=pltpu.VMEM)
+    return pl.pallas_call(
+        functools.partial(head_kernel, ne, nv),
+        out_shape=jax.ShapeDtypeStruct((8, 128), jnp.float32),
+        in_specs=[vm, vm, pl.BlockSpec(memory_space=pl.ANY)],
+        out_specs=vm,
+        scratch_shapes=[
+            pltpu.VMEM(lm_head.shape, jnp.bfloat16),
+            pltpu.VMEM((peers, tokens, width), jnp.bfloat16),
+            pltpu.VMEM((peers, 8, 128), jnp.float32),
+            dma((4,)),
+            dma((peers,)),
+            dma((peers,)),
+            dma((peers,)),
+            dma((peers,)),
+        ],
+        compiler_params=pltpu.CompilerParams(
+            collective_id=1, has_side_effects=True, vmem_limit_bytes=VMEM_BYTES - 2 * 1024 * 1024
+        ),
+        name="head",
+    )(own, targets, lm_head)
+
+
+def kernels_fit(sizes, resid, w_gate, lm_head):
+    ne, nv, nb = sizes
+    tokens, width = resid.shape[1:]
+    hidden_width = w_gate.shape[2]
+    rows = ne * nv * nb * tokens
+    need = 2 * (3 * width * hidden_width + rows * (3 * width + hidden_width) + 8 * ne * tokens * width)
+    group = ne * nv * tokens
+    head_need = 2 * (lm_head.shape[0] * width + 4 * group * width)
+    return (
+        nb % 2 == 0
+        and tokens % 8 == 0
+        and width % (128 * COLUMN_CHUNKS) == 0
+        and hidden_width % 256 == 0
+        and lm_head.shape[0] % 256 == 0
+        and group <= 128
+        and max(need, head_need) < VMEM_BYTES - 4 * 1024 * 1024
+    )
+
+
+def on_device_kernels(
+    sizes,
+    resid,
+    moe_gain,
+    final_gain,
+    router,
+    w_gate,
+    w_up,
+    w_down,
+    lm_head,
+    expert_ids,
+    target_ids,
+    choice_len,
+    choice_question,
+):
+    ne, nv, nb = sizes
+    stream = resid[0].astype(jnp.float32)
+    token_count = stream.shape[0]
+    normed_in = rms_scale(stream, moe_gain).astype(jnp.bfloat16)
+    router_logit = jnp.dot(normed_in, router, preferred_element_type=jnp.float32)
+    route_ids = expert_ids[0]
+    gate_weights = route_gates(router_logit, route_ids)
+    gates = jnp.sum(
+        jnp.where(
+            route_ids[:, :, None] == jnp.arange(ne, dtype=jnp.int32)[None, None, :],
+            gate_weights[:, :, None],
+            0.0,
+        ),
+        axis=1,
+    )
+    normed_out = experts_call(
+        sizes, normed_in, resid[0], gates, final_gain.reshape(1, -1), w_gate, w_up, w_down
+    )
+    targets = target_ids[0]
+    group_tokens = targets.shape[0]
+    found = head_call(sizes, normed_out, targets.reshape(-1, 1), lm_head)
+    group_logprob = found[0, :group_tokens]
+    lengths = choice_len[0]
+    positions = jnp.arange(group_tokens, dtype=jnp.int32)
+    choice_total = jnp.sum(
+        jnp.where(choice_member(lengths, positions), group_logprob[None, :], 0.0), axis=1
+    )
+    own_first = lax.axis_index(("expert", "vocab")) * token_count
+    own_logprob = lax.dynamic_slice_in_dim(group_logprob, own_first, token_count, 0)
+    choice_prob = choice_softmax(choice_total, lengths, choice_question[0])
+    return (own_logprob.reshape(1, -1), choice_prob.reshape(1, -1))
+
+
+def either(sizes, *arrays):
+    if kernels_fit(sizes, arrays[0], arrays[4], arrays[7]):
+        return on_device_kernels(sizes, *arrays)
+    return on_device(*arrays)
+
+
 def solution(mesh):
+    sizes = tuple(mesh.shape[axis] for axis in ("expert", "vocab", "batch"))
     return jax.shard_map(
-        on_device,
+        functools.partial(either, sizes),
         mesh=mesh,
         in_specs=(
             P("batch", ("expert", "vocab"), None),

time: 219 us -> 116 us (0.53)
  Pallas kernels: 0 us -> 107 us
  blocking collectives: 97.2 us -> 0 us
  waiting for transfers between devices: 40.2 us -> 0 us
  matrix products: 35.9 us -> 0.16 us
  between operations: 15.6 us -> 0.71 us
  starting transfers between devices: 14.8 us -> 0 us
  local copies, waits for them, and re-layouts: 9.43 us -> 2.06 us
    pallas_call x0 -> x2, Pallas kernels: none -> 107 us  [the longest x1 71.5 us: experts_call(): pl.pallas_call(functools.partial(experts_kernel, ne, nv, nb), out_shape=j...]
    unnamed x2 -> x0, blocking collectives: 47 us -> none
    dot_general x6 -> x1, matrix products: 35.9 us -> 0.16 us  [on_device_kernels(): jnp.dot(normed_in, router, preferred_element_type=jnp.float32)]
    all_gather x1 -> x0, blocking collectives: 32.4 us -> none  [on_device(): lax.all_gather(normed_out, ('expert', 'vocab'), axis=0, tiled=True)]
    all_gather x1 -> x0, waiting for transfers between devices: 28.1 us -> none  [on_device(): lax.all_gather(arrived, ('vocab', 'batch'), axis=0, tiled=True)]
    all_to_all x1 -> x0, blocking collectives: 17.8 us -> none  [on_device(): lax.all_to_all(buckets, 'expert', split_axis=0, concat_axis=0, tiled=True)]
    all_to_all x1 -> x0, waiting for transfers between devices: 11.2 us -> none  [on_device(): lax.all_to_all(outgoing, 'expert', split_axis=0, concat_axis=0, tiled=True)]
    unnamed x2 -> x0, starting transfers between devices: 10.2 us -> none
  transfers between devices with their start and end apart: 4 -> 0, of which waited for: 3 -> 0; matrix products, arithmetic and copies ran while one was open for 1% -> 0% of each run, Pallas kernels for 0% -> 0%
where the time goes in v1:
time: 116 us; the launch traced here: 115 us
  Pallas kernels  107 us (92%)
  other arithmetic  4.86 us (4%)
  local copies, waits for them, and re-layouts  2.06 us (2%)
    pallas_call x1, Pallas kernels, experts_call(): pl.pallas_call(functools.partial(experts_kernel, ne, nv, nb), out_shape=j...  71.5 us
    pallas_call x1, Pallas kernels, head_call(): pl.pallas_call(functools.partial(head_kernel, ne, nv), out_shape=jax.Shap...  35.9 us

profile of v1, /device:TPU:0, one launch (start us, length us, event | category | flops | bytes accessed | tf_op | source)
XLA Modules:
  0.0 115.2 jit_solution(9200512503490910527)
XLA Ops:
  0.6 0.0 copy-start
  0.6 1.1 fusion
  1.7 1.0 fusion.2.own_ref
  2.7 0.0 copy-done
  2.7 0.0 copy-start.1
  2.8 0.2 fusion.8
  2.9 0.7 select_reduce_fusion.2
  3.7 0.7 select_reduce_fusion.1
  4.4 0.7 copy.17.gates_ref
  5.0 0.0 copy-done.1
  5.0 0.0 copy-start.3
  5.0 71.5 %experts.1.own_ref = bf16[8,6144]{1,0:T(8,128)(2,1)} custom-call(bf16[8,6144]{1,0:T(8,128)(2,1)} %copy-done.1, bf16[8,6144]{1,0:T(8,128)(2,1)} %bitcast.31, f32[8,4]{1,0:T(8,128)} %copy.17.gates_ref, f32[1,6144]{1,0:T(1,128)} %bitcast.32, bf16[1,6144,1024]{2,1,0:T(8,128)(2,1)} %wg_hbm.1, bf16[1,6144,1024]{2,1,0:T(8,128)(2,1)} %wu_hbm.1, ...), custom_call_target="tpu_custom_call" | custom-call | tf_op jit(solution)/shard_map/experts/pallas_call | solution.py:379
  76.6 0.0 copy-done.3
  76.6 0.7 copy.18.target_ref
  77.3 0.0 copy-start.4
  77.3 0.0 copy-start.2
  77.3 35.9 %head.1 = f32[8,128]{1,0:T(8,128)} custom-call(bf16[8,6144]{1,0:T(8,128)(2,1)} %experts.1.own_ref, s32[64,1]{1,0:T(8,128)} %copy.18.target_ref, bf16[2048,6144]{1,0:T(8,128)(2,1)} %head_hbm.1), custom_call_target="tpu_custom_call" | custom-call | tf_op jit(solution)/shard_map/head/pallas_call | solution.py:513
  113.2 0.7 slice_bitcast_fusion
  113.9 0.0 copy-done.4
  113.9 0.2 reduce-window.7
  114.1 0.2 select_reduce_fusion
  114.3 0.0 copy-done.2
  114.3 0.2 fusion.3
  114.5 0.2 fusion.4
  114.7 0.6 bitcast_divide_fusion
  (6 shorter events, 0.1 us)
Async XLA Ops:
  0.6 2.1 %copy-start = (bf16[6144,4]{0,1:T(4,128)(2,1)S(1)}, bf16[6144,4]{0,1:T(4,128)(2,1)}, u32[]{:S(2)}) copy-start(bf16[6144,4]{0,1:T(4,128)(2,1)} %param.15) | copy-start | bytes 147460
  2.7 2.3 %copy-start.1 = (bf16[8,6144]{1,0:T(8,128)(2,1)}, bf16[8,6144]{1,0:T(8,128)(2,1)S(1)}, u32[]{:S(2)}) copy-start(bf16[8,6144]{1,0:T(8,128)(2,1)S(1)} %fusion.2.own_ref) | copy-start | bytes 294916
  5.0 71.6 %copy-start.3 = (s32[1,64]{1,0:T(1,128)S(1)}, s32[1,64]{1,0:T(1,128)}, u32[]{:S(2)}) copy-start(s32[1,64]{1,0:T(1,128)} %param.21) | copy-start | bytes 772
  77.3 36.6 %copy-start.4 = (s32[1,8]{1,0:T(1,128)S(1)}, s32[1,8]{1,0:T(1,128)}, u32[]{:S(2)}) copy-start(s32[1,8]{1,0:T(1,128)} %param.22) | copy-start | bytes 100
  77.3 37.0 %copy-start.2 = (s32[1,8]{1,0:T(1,128)S(1)}, s32[1,8]{1,0:T(1,128)}, u32[]{:S(2)}) copy-start(s32[1,8]{1,0:T(1,128)} %param.23) | copy-start | bytes 100

commit v2 on v1

--- a/solution.py
+++ b/solution.py
@@ -211,22 +211,18 @@
     rz_recv,
 ):
     e, v, b = lax.axis_index("expert"), lax.axis_index("vocab"), lax.axis_index("batch")
-    half = nb // 2
-    chips = nv * half
     core = lax.rem(b, 2)
     other = 1 - core
-    chip = v * half + b // 2
     tokens, width = own_ref.shape
     block = ne * tokens
+    chips = 4
+    across = (e, 1 - v, b)
+    along = (e, v, lax.rem(b + 2, 4))
+    mate = (e, v, b + 1 - 2 * core)
+    near = {1: along, 2: across}
 
     def at_expert(k):
         return (lax.rem(e + k, ne), v, b)
-
-    def at_chip(k):
-        c = lax.rem(chip + k, chips)
-        return (e, c // half, lax.rem(c, half) * 2 + core)
-
-    mate = (e, v, b + 1 - 2 * core)
 
     loads = [
         pltpu.make_async_copy(src, dst, w_sem.at[i])
@@ -234,9 +230,7 @@
     ]
     for load in loads:
         load.start()
-    greet(
-        [at_expert(k) for k in range(1, ne)] + [at_chip(k) for k in range(1, chips)] + [mate]
-    )
+    greet([at_expert(k) for k in range(1, ne)] + [across, along, mate])
 
     z_copies = [
         push(own_ref, zin.at[e], z_send.at[k], z_recv.at[k], at_expert(k)) for k in range(1, ne)
@@ -246,104 +240,149 @@
     zin[e] = own_ref[...]
     for copy in z_copies:
         copy.wait_recv()
-    xs[core, chip] = (
-        zin[...].astype(jnp.float32).reshape(block, width).astype(jnp.bfloat16)
-    )
-
-    c_copies = [
-        push(
-            xs.at[core, chip], xs.at[core, chip], c_send.at[k], c_recv.at[k], at_chip(k)
-        )
-        for k in range(1, chips)
-    ]
-    p_copies = []
-    for k in range(chips):
-        c = lax.rem(chip + chips - k, chips)
-        p_copies.append(push(xs.at[core, c], xs.at[core, c], p_send.at[k], p_recv.at[k], mate))
-    for copy in c_copies:
-        copy.start()
-    p_copies[0].start()
-    for k in range(1, chips):
-        c_copies[k - 1].wait_recv()
-        p_copies[k].start()
-    for copy in p_copies:
-        copy.wait_recv()
-
-    rows = 2 * chips * block
+    xs[0, core] = zin[...].astype(jnp.float32).reshape(block, width).astype(jnp.bfloat16)
+
+    part_width = width // 2
+
+    def piece(h):
+        return pl.ds(h * part_width, part_width)
+
+    def plane_push(src_slot, dst_slot, h, n):
+        return push(
+            xs.at[src_slot, core, :, piece(h)],
+            xs.at[dst_slot, core, :, piece(h)],
+            c_send.at[dst_slot, h],
+            c_recv.at[dst_slot, h],
+            near[n],
+        )
+
+    def mate_push(slot, h):
+        return push(
+            xs.at[slot, core, :, piece(h)],
+            xs.at[slot, core, :, piece(h)],
+            p_send.at[slot, h],
+            p_recv.at[slot, h],
+            mate,
+        )
+
+    c_copies = {(n, h): plane_push(0, n, h, n) for n in (1, 2) for h in (0, 1)}
+    c_copies[3, 0] = plane_push(2, 3, 0, 1)
+    c_copies[3, 1] = plane_push(1, 3, 1, 2)
+    p_copies = {(slot, h): mate_push(slot, h) for slot in range(4) for h in (0, 1)}
+    for key in ((2, 0), (1, 1), (2, 1), (1, 0)):
+        c_copies[key].start()
+    p_copies[0, 0].start()
+    p_copies[0, 1].start()
+    for key, follow in (((2, 0), (3, 0)), ((1, 1), (3, 1)), ((1, 0), None), ((2, 1), None)):
+        c_copies[key].wait_recv()
+        if follow is not None:
+            c_copies[follow].start()
+        p_copies[key].start()
+    hidden_width = wg.shape[1]
+    tile = min(256, hidden_width)
+    rows = 2 * block
+
+    def expand(first, count):
+        @pl.loop(0, hidden_width // tile)
+        def _(i):
+            cols = pl.ds(pl.multiple_of(i * tile, tile), tile)
+            x = xs[first : first + count].reshape(count * rows, width)
+            g = jnp.dot(x, wg[:, cols], preferred_element_type=jnp.float32)
+            u = jnp.dot(x, wu[:, cols], preferred_element_type=jnp.float32)
+            hid[first * rows : (first + count) * rows, cols] = (
+                g / (1.0 + jnp.exp(-g)) * u
+            ).astype(jnp.bfloat16)
+
     loads[0].wait()
     loads[1].wait()
-    hidden_width = wg.shape[1]
-    tile = min(256, hidden_width)
-
-    @pl.loop(0, hidden_width // tile)
-    def _(i):
-        cols = pl.ds(pl.multiple_of(i * tile, tile), tile)
-        x = xs[...].reshape(rows, width)
-        g = jnp.dot(x, wg[:, cols], preferred_element_type=jnp.float32)
-        u = jnp.dot(x, wu[:, cols], preferred_element_type=jnp.float32)
-        hid[:, cols] = (g / (1.0 + jnp.exp(-g)) * u).astype(jnp.bfloat16)
+    for slot in (0, 1):
+        for h in (0, 1):
+            p_copies[slot, h].wait_recv()
+    expand(0, 2)
+    for h in (0, 1):
+        c_copies[3, h].wait_recv()
+        p_copies[3, h].start()
+    for slot in (2, 3):
+        for h in (0, 1):
+            p_copies[slot, h].wait_recv()
+    expand(2, 2)
 
     loads[2].wait()
     chunk = width // COLUMN_CHUNKS
     down_tile = 512 if chunk % 512 == 0 else 128
-    rp, rc, rz = [], [], []
+    rp, rd, rn, rz = {}, {}, {}, {}
 
     def columns(j):
         return pl.ds(j * chunk, chunk)
+
+    def wide(ref_value):
+        return ref_value.astype(jnp.float32)
 
     def down(j):
         @pl.loop(0, chunk // down_tile)
         def _(i):
             cols = pl.ds(pl.multiple_of(j * chunk + i * down_tile, down_tile), down_tile)
             y = jnp.dot(hid[...], wd[:, cols], preferred_element_type=jnp.float32)
-            part[:, :, :, cols] = y.astype(jnp.bfloat16).reshape(2, chips, block, down_tile)
-
-        copy = push(
-            part.at[other, :, :, columns(j)],
+            part[:, :, :, cols] = y.astype(jnp.bfloat16).reshape(chips, 2, block, down_tile)
+
+        rp[j] = push(
+            part.at[:, other, :, columns(j)],
             rpair.at[:, :, columns(j)],
             rp_send.at[j],
             rp_recv.at[j],
             mate,
         )
-        copy.start()
-        rp.append(copy)
+        rp[j].start()
+
+    def neighbour_push(slot, j):
+        return push(
+            part.at[slot, core, :, columns(j)],
+            rchip.at[slot - 1, :, columns(j)],
+            rc_send.at[j, slot],
+            rc_recv.at[j, slot],
+            near[slot],
+        )
 
     def pair_sum(j):
         rp[j].wait_recv()
-        total = part[core, :, :, columns(j)].astype(jnp.float32) + rpair[
-            :, :, columns(j)
-        ].astype(jnp.float32)
-        part[core, :, :, columns(j)] = total.astype(jnp.bfloat16)
-        for k in range(1, chips):
-            to = lax.rem(chip + k, chips)
-            copy = push(
-                part.at[core, to, :, columns(j)],
-                rchip.at[k - 1, :, columns(j)],
-                rc_send.at[j, k],
-                rc_recv.at[j, k],
-                at_chip(k),
-            )
-            copy.start()
-            rc.append(copy)
+        total = wide(part[:, core, :, columns(j)]) + wide(rpair[:, :, columns(j)])
+        part[:, core, :, columns(j)] = total.astype(jnp.bfloat16)
+        via = 2 - j % 2
+        rd[j] = push(
+            part.at[3, core, :, columns(j)],
+            rchip.at[2, :, columns(j)],
+            rc_send.at[j, 3],
+            rc_recv.at[j, 3],
+            near[via],
+        )
+        rd[j].start()
+        rn[j, via] = neighbour_push(via, j)
+        rn[j, via].start()
+
+    def relay(j):
+        last = 1 + j % 2
+        rd[j].wait_recv()
+        total = wide(part[last, core, :, columns(j)]) + wide(rchip[2, :, columns(j)])
+        part[last, core, :, columns(j)] = total.astype(jnp.bfloat16)
+        rn[j, last] = neighbour_push(last, j)
+        rn[j, last].start()
 
     def plane_sum(j):
-        for k in range(1, chips):
-            rc[j * (chips - 1) + k - 1].wait_recv()
-        total = part[core, chip, :, columns(j)].astype(jnp.float32)
-        for k in range(1, chips):
-            total = total + rchip[k - 1, :, columns(j)].astype(jnp.float32)
+        rn[j, 1].wait_recv()
+        rn[j, 2].wait_recv()
+        total = wide(part[0, core, :, columns(j)])
+        total = total + wide(rchip[0, :, columns(j)]) + wide(rchip[1, :, columns(j)])
         zs[:, :, columns(j)] = total.reshape(ne, tokens, chunk).astype(jnp.bfloat16)
         for k in range(1, ne):
             to = lax.rem(e + k, ne)
-            copy = push(
+            rz[j, k] = push(
                 zs.at[to, :, columns(j)],
                 zo.at[e, :, columns(j)],
                 rz_send.at[j, k],
                 rz_recv.at[j, k],
                 at_expert(k),
             )
-            copy.start()
-            rz.append(copy)
+            rz[j, k].start()
         zo[e, :, columns(j)] = zs[e, :, columns(j)]
 
     for j in range(COLUMN_CHUNKS):
@@ -352,8 +391,11 @@
             pair_sum(j - 1)
     pair_sum(COLUMN_CHUNKS - 1)
     for j in range(COLUMN_CHUNKS):
-        plane_sum(j)
-    for copy in rz:
+        relay(j)
+        if j >= 1:
+            plane_sum(j - 1)
+    plane_sum(COLUMN_CHUNKS - 1)
+    for copy in rz.values():
         copy.wait_recv()
     gates = gates_ref[...]
     mixed = resid_ref[...].astype(jnp.float32)
@@ -361,7 +403,10 @@
         mixed = mixed + gates[:, k : k + 1] * zo[k].astype(jnp.float32)
     scale = lax.rsqrt(jnp.mean(mixed * mixed, axis=-1, keepdims=True) + epsilon)
     out_ref[...] = (mixed * scale * gain_ref[...]).astype(jnp.bfloat16)
-    for copy in z_copies + c_copies + p_copies + rp + rc + rz:
+    for group in (c_copies, p_copies, rp, rd, rn, rz):
+        for copy in group.values():
+            copy.wait_send()
+    for copy in z_copies:
         copy.wait_send()
 
 
@@ -386,9 +431,9 @@
             pltpu.VMEM((width, hidden_width), bf16),
             pltpu.VMEM((hidden_width, width), bf16),
             pltpu.VMEM((ne, tokens, width), bf16),
-            pltpu.VMEM((2, chips, block, width), bf16),
+            pltpu.VMEM((chips, 2, block, width), bf16),
             pltpu.VMEM((2 * chips * block, hidden_width), bf16),
-            pltpu.VMEM((2, chips, block, width), bf16),
+            pltpu.VMEM((chips, 2, block, width), bf16),
             pltpu.VMEM((chips, block, width), bf16),
             pltpu.VMEM((max(1, chips - 1), block, width), bf16),
             pltpu.VMEM((ne, tokens, width), bf16),
@@ -396,10 +441,10 @@
             dma((3,)),
             dma((ne,)),
             dma((ne,)),
-            dma((chips,)),
-            dma((chips,)),
-            dma((chips,)),
-            dma((chips,)),
+            dma((chips, 2)),
+            dma((chips, 2)),
+            dma((chips, 2)),
+            dma((chips, 2)),
             dma((n,)),
             dma((n,)),
             dma((n, chips)),
@@ -441,14 +486,25 @@
     for load in loads:
         load.start()
     greet([at(k) for k in range(1, peers)])
-    copies = [
-        push(own_ref, ys.at[me], y_send.at[k], y_recv.at[k], at(k)) for k in range(1, peers)
+    across = (e, 1 - v, b)
+    along = [
+        push(own_ref, ys.at[me], y_send.at[0, k], y_recv.at[0, k], (lax.rem(e + k, ne), v, b))
+        for k in range(1, ne)
     ]
-    for copy in copies:
+    turns = [push(own_ref, ys.at[me], y_send.at[1, 0], y_recv.at[1, 0], across)]
+    for k in range(1, ne):
+        slot = lax.rem(e + ne - k, ne) * nv + v
+        turns.append(push(ys.at[slot], ys.at[slot], y_send.at[1, k], y_recv.at[1, k], across))
+    for copy in along:
         copy.start()
+    turns[0].start()
     ys[me] = own_ref[...]
-    for copy in copies:
+    for k in [1] + [k for k in range(ne - 1, 1, -1)]:
+        along[k - 1].wait_recv()
+        turns[k].start()
+    for copy in turns:
         copy.wait_recv()
+    copies = along + turns
     for load in loads:
         load.wait()
     y = ys[...].astype(jnp.float32).reshape(rows, width).astype(jnp.bfloat16)
@@ -520,8 +576,8 @@
             pltpu.VMEM((peers, tokens, width), jnp.bfloat16),
             pltpu.VMEM((peers, 8, 128), jnp.float32),
             dma((4,)),
-            dma((peers,)),
-            dma((peers,)),
+            dma((2, ne)),
+            dma((2, ne)),
             dma((peers,)),
             dma((peers,)),
         ],
@@ -541,7 +597,8 @@
     group = ne * nv * tokens
     head_need = 2 * (lm_head.shape[0] * width + 4 * group * width)
     return (
-        nb % 2 == 0
+        nv == 2
+        and nb == 4
         and tokens % 8 == 0
         and width % (128 * COLUMN_CHUNKS) == 0
         and hidden_width % 256 == 0

time: 116 us -> 108 us (0.931)
  Pallas kernels: 107 us -> 99.6 us
    pallas_call x1, Pallas kernels: 71.5 us -> 66.3 us  [experts_call(): pl.pallas_call(functools.partial(experts_kernel, ne, nv, nb), out_shape=j...]
    pallas_call x1, Pallas kernels: 35.9 us -> 33.3 us  [head_call(): pl.pallas_call(functools.partial(head_kernel, ne, nv), out_shape=jax.Shap...]
where the time goes in v2:
time: 108 us; the launch traced here: 107 us
  Pallas kernels  99.6 us (92%)
  other arithmetic  4.86 us (5%)
  local copies, waits for them, and re-layouts  2.06 us (2%)
    pallas_call x1, Pallas kernels, experts_call(): pl.pallas_call(functools.partial(experts_kernel, ne, nv, nb), out_shape=j...  66.3 us
    pallas_call x1, Pallas kernels, head_call(): pl.pallas_call(functools.partial(head_kernel, ne, nv), out_shape=jax.Shap...  33.3 us

profile of v2, /device:TPU:0, one launch (start us, length us, event | category | flops | bytes accessed | tf_op | source)
XLA Modules:
  0.0 107.4 jit_solution(10771422433615355274)
XLA Ops:
  0.6 0.0 copy-start
  0.6 1.1 fusion
  1.7 1.0 fusion.2.own_ref
  2.7 0.0 copy-done
  2.7 0.0 copy-start.1
  2.8 0.2 fusion.8
  2.9 0.7 select_reduce_fusion.2
  3.7 0.7 select_reduce_fusion.1
  4.4 0.7 copy.17.gates_ref
  5.0 0.0 copy-done.1
  5.0 0.0 copy-start.3
  5.0 66.3 %experts.1.own_ref = bf16[8,6144]{1,0:T(8,128)(2,1)} custom-call(bf16[8,6144]{1,0:T(8,128)(2,1)} %copy-done.1, bf16[8,6144]{1,0:T(8,128)(2,1)} %bitcast.31, f32[8,4]{1,0:T(8,128)} %copy.17.gates_ref, f32[1,6144]{1,0:T(1,128)} %bitcast.32, bf16[1,6144,1024]{2,1,0:T(8,128)(2,1)} %wg_hbm.1, bf16[1,6144,1024]{2,1,0:T(8,128)(2,1)} %wu_hbm.1, ...), custom_call_target="tpu_custom_call" | custom-call | tf_op jit(solution)/shard_map/experts/pallas_call | solution.py:424
  71.3 0.0 copy-done.3
  71.3 0.7 copy.18.target_ref
  72.0 0.0 copy-start.4
  72.0 0.0 copy-start.2
  72.1 33.3 %head.1 = f32[8,128]{1,0:T(8,128)} custom-call(bf16[8,6144]{1,0:T(8,128)(2,1)} %experts.1.own_ref, s32[64,1]{1,0:T(8,128)} %copy.18.target_ref, bf16[2048,6144]{1,0:T(8,128)(2,1)} %head_hbm.1), custom_call_target="tpu_custom_call" | custom-call | tf_op jit(solution)/shard_map/head/pallas_call | solution.py:569
  105.4 0.7 slice_bitcast_fusion
  106.0 0.0 copy-done.4
  106.0 0.2 reduce-window.7
  106.2 0.2 select_reduce_fusion
  106.4 0.0 copy-done.2
  106.4 0.2 fusion.3
  106.6 0.2 fusion.4
  106.8 0.6 bitcast_divide_fusion
  (6 shorter events, 0.1 us)
Async XLA Ops:
  0.6 2.1 %copy-start = (bf16[6144,4]{0,1:T(4,128)(2,1)S(1)}, bf16[6144,4]{0,1:T(4,128)(2,1)}, u32[]{:S(2)}) copy-start(bf16[6144,4]{0,1:T(4,128)(2,1)} %param.15) | copy-start | bytes 147460
  2.7 2.3 %copy-start.1 = (bf16[8,6144]{1,0:T(8,128)(2,1)}, bf16[8,6144]{1,0:T(8,128)(2,1)S(1)}, u32[]{:S(2)}) copy-start(bf16[8,6144]{1,0:T(8,128)(2,1)S(1)} %fusion.2.own_ref) | copy-start | bytes 294916
  5.0 66.3 %copy-start.3 = (s32[1,64]{1,0:T(1,128)S(1)}, s32[1,64]{1,0:T(1,128)}, u32[]{:S(2)}) copy-start(s32[1,64]{1,0:T(1,128)} %param.21) | copy-start | bytes 772
  72.0 34.0 %copy-start.4 = (s32[1,8]{1,0:T(1,128)S(1)}, s32[1,8]{1,0:T(1,128)}, u32[]{:S(2)}) copy-start(s32[1,8]{1,0:T(1,128)} %param.22) | copy-start | bytes 100
  72.0 34.4 %copy-start.2 = (s32[1,8]{1,0:T(1,128)S(1)}, s32[1,8]{1,0:T(1,128)}, u32[]{:S(2)}) copy-start(s32[1,8]{1,0:T(1,128)} %param.23) | copy-start | bytes 100
